TPU v7x, 32 devices: a whole 2x2x4 slice. The times are simulated.
32 devices in a mesh: batch: 4 (over z), cols: 8 (over y, x, core).
Axes of the slice: x: 2, y: 2, z: 4, core: 2. Of those that a mesh axis runs over, the one named last changes fastest.
Arguments:
- grad_up: float32 [4, 1024, 4096], P('batch', None, 'cols'), may hold values from -0.875 to 0.875
- grad_down: float32 [4, 4096, 1024], P('batch', 'cols'), may hold values from -0.875 to 0.875
- grad_query: float32 [4, 1024, 1024], P('batch', None, 'cols'), may hold values from -0.875 to 0.875
- grad_key: float32 [4, 1024, 1024], P('batch', None, 'cols'), may hold values from -0.875 to 0.875
- grad_value: float32 [4, 1024, 1024], P('batch', None, 'cols'), may hold values from -0.875 to 0.875
- grad_mixed: float32 [4, 1024, 1024], P('batch', 'cols'), may hold values from -0.875 to 0.875
- grad_norm: float32 [4, 1024], P('batch'), may hold values from -8 to 8
- grad_bias: float32 [4, 1024], P('batch'), may hold values from -8 to 8
- weight_up: float32 [1024, 4096], P('batch', 'cols'), may hold values from -0.25 to 0.25
- weight_down: float32 [4096, 1024], P('cols', 'batch'), may hold values from -0.125 to 0.125
- weight_query: float32 [1024, 1024], P('batch', 'cols'), may hold values from -0.25 to 0.25
- weight_key: float32 [1024, 1024], P('batch', 'cols'), may hold values from -0.25 to 0.25
- weight_value: float32 [1024, 1024], P('batch', 'cols'), may hold values from -0.25 to 0.25
- weight_mixed: float32 [1024, 1024], P('cols', 'batch'), may hold values from -0.25 to 0.25
- weight_norm: float32 [1024], P('batch'), may hold values from 0.25 to 1.75
- weight_bias: float32 [1024], P('batch'), may hold values from -3 to 3
- moment_up: float32 [1024, 4096], P('batch', 'cols'), may hold values from -0.1875 to 0.1875
- moment_down: float32 [4096, 1024], P('cols', 'batch'), may hold values from -0.09375 to 0.09375
- moment_query: float32 [1024, 1024], P('batch', 'cols'), may hold values from -0.1875 to 0.1875
- moment_key: float32 [1024, 1024], P('batch', 'cols'), may hold values from -0.1875 to 0.1875
- moment_value: float32 [1024, 1024], P('batch', 'cols'), may hold values from -0.1875 to 0.1875
- moment_mixed: float32 [1024, 1024], P('cols', 'batch'), may hold values from -0.1875 to 0.1875
- moment_norm: float32 [1024], P('batch'), may hold values from -1.75 to 1.75
- moment_bias: float32 [1024], P('batch'), may hold values from -1.75 to 1.75
Outputs:
- copy_up: bfloat16 [1024, 4096], P(None, 'cols')
- copy_down: bfloat16 [4096, 1024], P('cols')
- copy_query: bfloat16 [1024, 1024], P(None, 'cols')
- copy_key: bfloat16 [1024, 1024], P(None, 'cols')
- copy_value: bfloat16 [1024, 1024], P(None, 'cols')
- copy_mixed: bfloat16 [1024, 1024], P('cols')
- copy_norm: bfloat16 [1024], replicated
- copy_bias: bfloat16 [1024], replicated
- new_up: float32 [1024, 4096], P('batch', 'cols')
- new_down: float32 [4096, 1024], P('cols', 'batch')
- new_query: float32 [1024, 1024], P('batch', 'cols')
- new_key: float32 [1024, 1024], P('batch', 'cols')
- new_value: float32 [1024, 1024], P('batch', 'cols')
- new_mixed: float32 [1024, 1024], P('cols', 'batch')
- new_norm: float32 [1024], P('batch')
- new_bias: float32 [1024], P('batch')
- state_new_up: float32 [1024, 4096], P('batch', 'cols')
- state_new_down: float32 [4096, 1024], P('cols', 'batch')
- state_new_query: float32 [1024, 1024], P('batch', 'cols')
- state_new_key: float32 [1024, 1024], P('batch', 'cols')
- state_new_value: float32 [1024, 1024], P('batch', 'cols')
- state_new_mixed: float32 [1024, 1024], P('cols', 'batch')
- state_new_norm: float32 [1024], P('batch')
- state_new_bias: float32 [1024], P('batch')
All inputs are finite; a program needn't handle non-finite values.
Results may differ from a plain program's by a relative error of at most 0.001.
Values may be sent and summed in bfloat16 or wider, within the bound.
A program may use at most 64 MiB of HBM per device.

v0:
```python
import jax
import jax.numpy as jnp
from jax import lax
from jax.sharding import PartitionSpec as P

learn_rate = 0.4
hold_rate = 0.9


def local(
    grad_up,
    grad_down,
    grad_query,
    grad_key,
    grad_value,
    grad_mixed,
    grad_norm,
    grad_bias,
    weight_up,
    weight_down,
    weight_query,
    weight_key,
    weight_value,
    weight_mixed,
    weight_norm,
    weight_bias,
    moment_up,
    moment_down,
    moment_query,
    moment_key,
    moment_value,
    moment_mixed,
    moment_norm,
    moment_bias,
):
    mean_up, mean_down, mean_query, mean_key, mean_value, mean_mixed = (
        lax.psum_scatter(grad_up[0], "batch", scatter_dimension=0, tiled=True),
        lax.psum_scatter(grad_down[0], "batch", scatter_dimension=1, tiled=True),
        lax.psum_scatter(grad_query[0], "batch", scatter_dimension=0, tiled=True),
        lax.psum_scatter(grad_key[0], "batch", scatter_dimension=0, tiled=True),
        lax.psum_scatter(grad_value[0], "batch", scatter_dimension=0, tiled=True),
        lax.psum_scatter(grad_mixed[0], "batch", scatter_dimension=1, tiled=True),
    )
    whole_norm, whole_bias = lax.psum((grad_norm[0], grad_bias[0]), "batch")
    place = lax.axis_index("batch")
    mean_norm = lax.dynamic_slice_in_dim(
        whole_norm, place * weight_norm.shape[0], weight_norm.shape[0]
    )
    mean_bias = lax.dynamic_slice_in_dim(
        whole_bias, place * weight_bias.shape[0], weight_bias.shape[0]
    )
    mean_rate = lax.axis_size("batch") ** (-0.5)
    mean_up = mean_up * mean_rate
    mean_down = mean_down * mean_rate
    mean_query = mean_query * mean_rate
    mean_key = mean_key * mean_rate
    mean_value = mean_value * mean_rate
    mean_mixed = mean_mixed * mean_rate
    mean_norm = mean_norm * mean_rate
    mean_bias = mean_bias * mean_rate
    (
        own_up,
        own_down,
        own_query,
        own_key,
        own_value,
        own_mixed,
        slope_up_norm,
        slope_down_norm,
        slope_query_norm,
        slope_key_norm,
        slope_value_norm,
        slope_mixed_norm,
    ) = lax.psum(
        (
            jnp.sum(weight_up * weight_up, axis=1, keepdims=True),
            jnp.sum(weight_down * weight_down, axis=0, keepdims=True),
            jnp.sum(weight_query * weight_query, axis=1, keepdims=True),
            jnp.sum(weight_key * weight_key, axis=1, keepdims=True),
            jnp.sum(weight_value * weight_value, axis=1, keepdims=True),
            jnp.sum(weight_mixed * weight_mixed, axis=0, keepdims=True),
            jnp.sum(mean_up * mean_up, axis=1, keepdims=True),
            jnp.sum(mean_down * mean_down, axis=0, keepdims=True),
            jnp.sum(mean_query * mean_query, axis=1, keepdims=True),
            jnp.sum(mean_key * mean_key, axis=1, keepdims=True),
            jnp.sum(mean_value * mean_value, axis=1, keepdims=True),
            jnp.sum(mean_mixed * mean_mixed, axis=0, keepdims=True),
        ),
        "cols",
    )
    mean_up = mean_up * (jnp.sqrt(own_up) * lax.rsqrt(slope_up_norm + 1e-06))
    mean_down = mean_down * (jnp.sqrt(own_down) * lax.rsqrt(slope_down_norm + 1e-06))
    mean_query = mean_query * (jnp.sqrt(own_query) * lax.rsqrt(slope_query_norm + 1e-06))
    mean_key = mean_key * (jnp.sqrt(own_key) * lax.rsqrt(slope_key_norm + 1e-06))
    mean_value = mean_value * (jnp.sqrt(own_value) * lax.rsqrt(slope_value_norm + 1e-06))
    mean_mixed = mean_mixed * (jnp.sqrt(own_mixed) * lax.rsqrt(slope_mixed_norm + 1e-06))
    state_new_up = hold_rate * moment_up + mean_up
    new_up = weight_up - learn_rate * state_new_up
    state_new_down = hold_rate * moment_down + mean_down
    new_down = weight_down - learn_rate * state_new_down
    state_new_query = hold_rate * moment_query + mean_query
    new_query = weight_query - learn_rate * state_new_query
    state_new_key = hold_rate * moment_key + mean_key
    new_key = weight_key - learn_rate * state_new_key
    state_new_value = hold_rate * moment_value + mean_value
    new_value = weight_value - learn_rate * state_new_value
    state_new_mixed = hold_rate * moment_mixed + mean_mixed
    new_mixed = weight_mixed - learn_rate * state_new_mixed
    state_new_norm = hold_rate * moment_norm + mean_norm
    new_norm = weight_norm - learn_rate * state_new_norm
    state_new_bias = hold_rate * moment_bias + mean_bias
    new_bias = weight_bias - learn_rate * state_new_bias
    copy_up, copy_down, copy_query, copy_key, copy_value, copy_mixed, copy_norm, copy_bias = (
        lax.all_gather(new_up.astype(jnp.bfloat16), "batch", axis=0, tiled=True),
        lax.all_gather(new_down.astype(jnp.bfloat16), "batch", axis=1, tiled=True),
        lax.all_gather(new_query.astype(jnp.bfloat16), "batch", axis=0, tiled=True),
        lax.all_gather(new_key.astype(jnp.bfloat16), "batch", axis=0, tiled=True),
        lax.all_gather(new_value.astype(jnp.bfloat16), "batch", axis=0, tiled=True),
        lax.all_gather(new_mixed.astype(jnp.bfloat16), "batch", axis=1, tiled=True),
        lax.all_gather(new_norm.astype(jnp.bfloat16), "batch", axis=0, tiled=True),
        lax.all_gather(new_bias.astype(jnp.bfloat16), "batch", axis=0, tiled=True),
    )
    return (
        copy_up,
        copy_down,
        copy_query,
        copy_key,
        copy_value,
        copy_mixed,
        copy_norm,
        copy_bias,
        new_up,
        new_down,
        new_query,
        new_key,
        new_value,
        new_mixed,
        new_norm,
        new_bias,
        state_new_up,
        state_new_down,
        state_new_query,
        state_new_key,
        state_new_value,
        state_new_mixed,
        state_new_norm,
        state_new_bias,
    )


def solution(mesh):
    placed = (
        P("batch", None, "cols"),
        P("batch", "cols", None),
        P("batch", None, "cols"),
        P("batch", None, "cols"),
        P("batch", None, "cols"),
        P("batch", "cols", None),
        P("batch", None),
        P("batch", None),
        P("batch", "cols"),
        P("cols", "batch"),
        P("batch", "cols"),
        P("batch", "cols"),
        P("batch", "cols"),
        P("cols", "batch"),
        P("batch"),
        P("batch"),
        P("batch", "cols"),
        P("cols", "batch"),
        P("batch", "cols"),
        P("batch", "cols"),
        P("batch", "cols"),
        P("cols", "batch"),
        P("batch"),
        P("batch"),
    )
    return jax.shard_map(
        local,
        mesh=mesh,
        in_specs=placed,
        out_specs=(
            P(None, "cols"),
            P("cols", None),
            P(None, "cols"),
            P(None, "cols"),
            P(None, "cols"),
            P("cols", None),
            P(),
            P(),
            P("batch", "cols"),
            P("cols", "batch"),
            P("batch", "cols"),
            P("batch", "cols"),
            P("batch", "cols"),
            P("cols", "batch"),
            P("batch"),
            P("batch"),
            P("batch", "cols"),
            P("cols", "batch"),
            P("batch", "cols"),
            P("batch", "cols"),
            P("batch", "cols"),
            P("cols", "batch"),
            P("batch"),
            P("batch"),
        ),
        check_vma=False,
    )
```

profile of v0, /device:TPU:0, one launch (start us, length us, event | category | flops | bytes accessed | tf_op | source)
XLA Modules:
  0.0 325.4 jit_solution(3272128390508653159)
XLA Ops:
  7.2 0.0 reduce-scatter.11.cloned.1.call-start
  7.2 0.7 reduce-scatter.11.cloned.1.call-update
  7.9 0.0 reduce-scatter.13.cloned.1.call-start
  8.0 0.7 reduce-scatter.13.cloned.1.call-update
  8.7 0.0 reduce-scatter.15.cloned.1.call-start
  8.7 0.7 reduce-scatter.15.cloned.1.call-update
  9.4 0.0 reduce-scatter.17.cloned.1.call-start
  9.5 0.5 reduce-scatter.17.cloned.1.call-update
  10.0 0.0 reduce-scatter.7.cloned.1.call-start
  10.1 0.5 reduce-scatter.7.cloned.1.call-update
  10.6 0.0 reduce-scatter.9.cloned.1.call-start
  10.6 0.5 reduce-scatter.9.cloned.1.call-update
  11.2 0.0 all-gather.7.cloned.1.call-start
  11.2 0.1 multiply_reduce_fusion.9
  11.4 0.1 multiply_reduce_fusion.7
  11.5 0.1 multiply_reduce_fusion.11
  11.7 0.1 multiply_reduce_fusion.3
  11.8 0.1 multiply_reduce_fusion.1
  11.9 23.0 %reduce-scatter.11.cloned.1.call-done = f32[256,128]{1,0:T(8,128)} async-done(((f32[1024,128]{1,0:T(8,128)}), f32[256,128]{1,0:T(8,128)}) %reduce-scatter.11.cloned.1.call-update) | async-done | bytes 131088 | tf_op jit(solution)/shard_map/reduce_scatter | solution.py:39
  34.9 1.0 multiply_reduce_fusion.10
  35.9 21.4 %reduce-scatter.13.cloned.1.call-done = f32[256,128]{1,0:T(8,128)} async-done(((f32[1024,128]{1,0:T(8,128)}), f32[256,128]{1,0:T(8,128)}) %reduce-scatter.13.cloned.1.call-update) | async-done | bytes 131088 | tf_op jit(solution)/shard_map/reduce_scatter | solution.py:40
  57.3 1.0 multiply_reduce_fusion.8
  58.3 21.4 %reduce-scatter.15.cloned.1.call-done = f32[256,128]{1,0:T(8,128)} async-done(((f32[1024,128]{1,0:T(8,128)}), f32[256,128]{1,0:T(8,128)}) %reduce-scatter.15.cloned.1.call-update) | async-done | bytes 131088 | tf_op jit(solution)/shard_map/reduce_scatter | solution.py:41
  79.8 1.0 multiply_reduce_fusion.6
  80.8 21.3 %reduce-scatter.17.cloned.1.call-done = f32[128,256]{1,0:T(8,128)} async-done(((f32[128,1024]{1,0:T(8,128)}), f32[128,256]{1,0:T(8,128)}) %reduce-scatter.17.cloned.1.call-update) | async-done | bytes 131088 | tf_op jit(solution)/shard_map/reduce_scatter | solution.py:42
  102.0 0.9 multiply_reduce_fusion.4
  103.0 0.0 copy-start.19
  103.0 0.0 copy-start.20
  103.0 0.0 copy-start.21
  103.0 0.0 copy-start.22
  103.0 0.0 copy-start.23
  103.0 0.0 copy-start.13
  103.0 43.1 %reduce-scatter.7.cloned.1.call-done = f32[256,512]{1,0:T(8,128)} async-done(((f32[1024,512]{1,0:T(8,128)}), f32[256,512]{1,0:T(8,128)}) %reduce-scatter.7.cloned.1.call-update) | async-done | bytes 524304 | tf_op jit(solution)/shard_map/reduce_scatter | solution.py:37
  146.1 1.2 multiply_reduce_fusion.2
  147.3 43.8 %reduce-scatter.9.cloned.1.call-done = f32[512,256]{1,0:T(8,128)} async-done(((f32[512,1024]{1,0:T(8,128)}), f32[512,256]{1,0:T(8,128)}) %reduce-scatter.9.cloned.1.call-update) | async-done | bytes 524304 | tf_op jit(solution)/shard_map/reduce_scatter | solution.py:38
  191.1 1.1 multiply_reduce_fusion
  192.2 23.6 %all-reduce = (f32[256,1]{0,1:T(1,128)S(1)}, f32[256,1]{0,1:T(1,128)S(1)}, f32[1,256]{1,0:T(1,128)S(1)}, f32[1,256]{1,0:T(1,128)S(1)}, f32[256,1]{0,1:T(1,128)S(...) all-reduce(f32[256,1]{0,1:T(1,128)S(1)} %bitcast.48, ...), channel_id=1, replica_groups=mesh['batch'=4,'cols'=8] {'cols'}, use_global_device_ids=true, to_apply=%region_4.0 | all-reduce | flops 3072 | bytes 24576 | tf_op jit(solution)/shard_map/psum | solution.py:74
  215.9 2.2 fusion.6
  218.1 0.0 all-gather.7.cloned.1.call-update
  218.1 0.0 all-gather.5.cloned.1.call-start
  218.2 10.5 %all-reduce.1 = (f32[1024]{0:T(1024)S(1)}, f32[1024]{0:T(1024)S(1)}) all-reduce(f32[1024]{0:T(1024)S(1)} %bitcast.56, f32[1024]{0:T(1024)S(1)} %bitcast.57), channel_id=1, replica_groups=mesh['batch'=4,'cols'=8] {'batch'}, use_global_device_ids=true, to_apply=%region_30.0 | all-reduce | flops 2048 | bytes 16384 | tf_op jit(solution)/shard_map/psum | solution.py:44
  228.8 0.7 fusion
  229.4 7.8 %all-gather = bf16[4,1,256]{2,1,0:T(2,128)(2,1)S(1)} all-gather(bf16[1,1,256]{2,1,0:T(2,128)(2,1)S(1)} %reshape.60), channel_id=1, replica_groups=mesh['batch'=4,'cols'=8] {'batch'}, dimensions={0}, use_global_device_ids=true | all-gather | bytes 2560 | tf_op jit(solution)/shard_map/all_gather | solution.py:120
  237.3 0.6 copy.48
  237.9 9.5 %all-gather.1 = bf16[4,1,256]{2,1,0:T(2,128)(2,1)S(1)} all-gather(bf16[1,1,256]{2,1,0:T(2,128)(2,1)S(1)} %reshape.62), channel_id=1, replica_groups=mesh['batch'=4,'cols'=8] {'batch'}, dimensions={0}, use_global_device_ids=true | all-gather | bytes 2560 | tf_op jit(solution)/shard_map/all_gather | solution.py:121
  247.4 0.6 copy.49
  248.0 0.0 copy-start.15
  248.1 0.0 copy-start.16
  248.1 1.2 fusion.7
  249.3 0.0 all-gather.5.cloned.1.call-update
  249.4 0.8 fusion.4
  250.2 16.1 %all_gather.27 = bf16[1024,128]{1,0:T(8,128)(2,1)S(1)} all-gather(bf16[256,128]{1,0:T(8,128)(2,1)S(1)} %get-tuple-element.50), channel_id=1, replica_groups=mesh['batch'=4,'cols'=8] {'batch'}, dimensions={0}, use_global_device_ids=true | all-gather | bytes 327680 | tf_op jit(solution)/shard_map/all_gather | solution.py:117
  266.3 0.8 fusion.3
  267.1 16.0 %all_gather.28 = bf16[1024,128]{1,0:T(8,128)(2,1)S(1)} all-gather(bf16[256,128]{1,0:T(8,128)(2,1)S(1)} %get-tuple-element.47), channel_id=1, replica_groups=mesh['batch'=4,'cols'=8] {'batch'}, dimensions={0}, use_global_device_ids=true | all-gather | bytes 327680 | tf_op jit(solution)/shard_map/all_gather | solution.py:118
  283.2 0.7 fusion.2
  283.9 13.9 %all_gather.29 = bf16[128,1024]{1,0:T(8,128)(2,1)S(1)} all-gather(bf16[128,256]{1,0:T(8,128)(2,1)S(1)} %get-tuple-element.44), channel_id=1, replica_groups=mesh['batch'=4,'cols'=8] {'batch'}, dimensions={1}, use_global_device_ids=true | all-gather | bytes 327680 | tf_op jit(solution)/shard_map/all_gather | solution.py:119
  297.8 0.8 fusion.5
  298.6 13.8 %all_gather.26 = bf16[1024,128]{1,0:T(8,128)(2,1)S(1)} all-gather(bf16[256,128]{1,0:T(8,128)(2,1)S(1)} %get-tuple-element.53), channel_id=1, replica_groups=mesh['batch'=4,'cols'=8] {'batch'}, dimensions={0}, use_global_device_ids=true | all-gather | bytes 327680 | tf_op jit(solution)/shard_map/all_gather | solution.py:116
  312.4 2.4 copy.56
  314.7 1.0 copy.57
  315.7 0.7 copy.58
  316.4 0.7 copy.59
  317.1 0.7 copy.60
  317.8 0.7 copy.61
  (50 shorter events, 0.2 us)
Async XLA Ops:
  7.2 27.7 %reduce-scatter.11.cloned.1.call-start = ((), (), s32[]{:S(2)}) async-start(), calls=%async_computation.10 | async-start | bytes 655360 | tf_op jit(solution)/shard_map/reduce_scatter | solution.py:39
  7.9 49.4 %reduce-scatter.13.cloned.1.call-start = ((), (), s32[]{:S(2)}) async-start(), calls=%async_computation.11 | async-start | bytes 655360 | tf_op jit(solution)/shard_map/reduce_scatter | solution.py:40
  8.7 71.1 %reduce-scatter.15.cloned.1.call-start = ((), (), s32[]{:S(2)}) async-start(), calls=%async_computation.12 | async-start | bytes 655360 | tf_op jit(solution)/shard_map/reduce_scatter | solution.py:41
  9.4 92.6 %reduce-scatter.17.cloned.1.call-start = ((), (), s32[]{:S(2)}) async-start(), calls=%async_computation.13 | async-start | bytes 655360 | tf_op jit(solution)/shard_map/reduce_scatter | solution.py:42
  10.0 136.1 %reduce-scatter.7.cloned.1.call-start = ((), (), s32[]{:S(2)}) async-start(), calls=%async_computation.6 | async-start | bytes 2621440 | tf_op jit(solution)/shard_map/reduce_scatter | solution.py:37
  10.0 1.2 copy-start.4
  10.0 1.3 copy-start.5
  10.1 1.4 copy-start.6
  10.1 1.5 copy-start.7
  10.1 1.6 copy-start.1
  10.6 1.2 copy-start
  10.6 180.5 %reduce-scatter.9.cloned.1.call-start = ((), (), s32[]{:S(2)}) async-start(), calls=%async_computation.8 | async-start | bytes 2621440 | tf_op jit(solution)/shard_map/reduce_scatter | solution.py:38
  11.2 204.7 %copy-start.12 = (f32[512,256]{1,0:T(8,128)S(1)}, f32[512,256]{1,0:T(8,128)}, u32[]{:S(2)}) copy-start(f32[512,256]{1,0:T(8,128)} %param.41) | copy-start | bytes 1572868
  11.2 301.2 %all-gather.7.cloned.1.call-start = ((), (), s32[]{:S(2)}) async-start(), calls=%async_computation.9 | async-start | bytes 1310720 | tf_op jit(solution)/shard_map/all_gather | solution.py:115
  103.0 115.2 %copy-start.18 = (f32[1,1024]{1,0:T(1,128)S(1)}, f32[1,1024]{1,0:T(1,128)}, u32[]{:S(2)}) copy-start(f32[1,1024]{1,0:T(1,128)} %param.30) | copy-start | bytes 12292
  103.0 115.2 %copy-start.19 = (f32[1,1024]{1,0:T(1,128)S(1)}, f32[1,1024]{1,0:T(1,128)}, u32[]{:S(2)}) copy-start(f32[1,1024]{1,0:T(1,128)} %param.31) | copy-start | bytes 12292
  103.0 125.7 %copy-start.20 = (f32[256]{0:T(256)S(1)}, f32[256]{0:T(256)}, u32[]{:S(2)}) copy-start(f32[256]{0:T(256)} %param.39) | copy-start | bytes 3076
  103.0 125.7 %copy-start.21 = (f32[256]{0:T(256)S(1)}, f32[256]{0:T(256)}, u32[]{:S(2)}) copy-start(f32[256]{0:T(256)} %param.47) | copy-start | bytes 3076
  103.0 125.7 %copy-start.22 = (f32[256]{0:T(256)S(1)}, f32[256]{0:T(256)}, u32[]{:S(2)}) copy-start(f32[256]{0:T(256)} %param.38) | copy-start | bytes 3076
  103.0 125.7 %copy-start.23 = (f32[256]{0:T(256)S(1)}, f32[256]{0:T(256)}, u32[]{:S(2)}) copy-start(f32[256]{0:T(256)} %param.46) | copy-start | bytes 3076
  103.0 145.0 %copy-start.13 = (f32[256,512]{1,0:T(8,128)S(1)}, f32[256,512]{1,0:T(8,128)}, u32[]{:S(2)}) copy-start(f32[256,512]{1,0:T(8,128)} %param.40) | copy-start | bytes 1572868
  146.1 101.9 %copy-start.2 = (f32[256,512]{1,0:T(8,128)S(1)}, f32[256,512]{1,0:T(8,128)}, u32[]{:S(2)}) copy-start(f32[256,512]{1,0:T(8,128)} %reduce-scatter.7.cloned.1.call-done) | copy-start | bytes 1572868
  218.1 31.3 %copy-start.9 = (f32[256,128]{1,0:T(8,128)S(1)}, f32[256,128]{1,0:T(8,128)}, u32[]{:S(2)}) copy-start(f32[256,128]{1,0:T(8,128)} %reduce-scatter.13.cloned.1.call-done) | copy-start | bytes 393220
  218.1 31.3 %copy-start.14 = (f32[256,128]{1,0:T(8,128)S(1)}, f32[256,128]{1,0:T(8,128)}, u32[]{:S(2)}) copy-start(f32[256,128]{1,0:T(8,128)} %param.43) | copy-start | bytes 393220
  218.1 94.3 %all-gather.5.cloned.1.call-start = ((), (), s32[]{:S(2)}) async-start(), calls=%async_computation.7 | async-start | bytes 1310720 | tf_op jit(solution)/shard_map/all_gather | solution.py:114
  248.0 18.3 %copy-start.10 = (f32[256,128]{1,0:T(8,128)S(1)}, f32[256,128]{1,0:T(8,128)}, u32[]{:S(2)}) copy-start(f32[256,128]{1,0:T(8,128)} %reduce-scatter.15.cloned.1.call-done) | copy-start | bytes 393220
  248.0 18.3 %copy-start.15 = (f32[256,128]{1,0:T(8,128)S(1)}, f32[256,128]{1,0:T(8,128)}, u32[]{:S(2)}) copy-start(f32[256,128]{1,0:T(8,128)} %param.44) | copy-start | bytes 393220
  248.1 35.1 %copy-start.11 = (f32[128,256]{1,0:T(8,128)S(1)}, f32[128,256]{1,0:T(8,128)}, u32[]{:S(2)}) copy-start(f32[128,256]{1,0:T(8,128)} %reduce-scatter.17.cloned.1.call-done) | copy-start | bytes 393220
  248.1 35.1 %copy-start.16 = (f32[128,256]{1,0:T(8,128)S(1)}, f32[128,256]{1,0:T(8,128)}, u32[]{:S(2)}) copy-start(f32[128,256]{1,0:T(8,128)} %param.45) | copy-start | bytes 393220
  249.3 48.5 %copy-start.8 = (f32[256,128]{1,0:T(8,128)S(1)}, f32[256,128]{1,0:T(8,128)}, u32[]{:S(2)}) copy-start(f32[256,128]{1,0:T(8,128)} %reduce-scatter.11.cloned.1.call-done) | copy-start | bytes 393220
  249.3 48.5 %copy-start.17 = (f32[256,128]{1,0:T(8,128)S(1)}, f32[256,128]{1,0:T(8,128)}, u32[]{:S(2)}) copy-start(f32[256,128]{1,0:T(8,128)} %param.42) | copy-start | bytes 393220
  312.4 2.4 copy-start.3
Sparse Core Ops, SparseCore 0:
  10.3 24.5 reduce-scatter.10
  37.1 20.1 reduce-scatter.12
  59.6 20.1 reduce-scatter.14
  81.9 20.1 reduce-scatter.16
  104.2 41.8 reduce-scatter.6
  148.3 42.8 reduce-scatter.8
  218.2 28.6 all-gather.6
  249.4 33.2 all-gather.4
where the time goes:
time: 326 us; the launch traced here: 325 us
  waiting for transfers between devices  178 us (55%)
  blocking collectives  111 us (34%)
  between operations  14.5 us (4%)
  other arithmetic  14.2 us (4%)
  local copies, waits for them, and re-layouts  7.42 us (2%)
    reduce_scatter x1, waiting for transfers between devices, local(): lax.psum_scatter(grad_down[0], 'batch', scatter_dimension=1, tiled=True)  43.8 us
    reduce_scatter x1, waiting for transfers between devices, local(): lax.psum_scatter(grad_up[0], 'batch', scatter_dimension=0, tiled=True)  43.1 us
    psum x1, blocking collectives, local(): lax.psum((jnp.sum(weight_up * weight_up, axis=1, keepdims=True), jnp.sum(...  23.6 us
    reduce_scatter x1, waiting for transfers between devices, local(): lax.psum_scatter(grad_query[0], 'batch', scatter_dimension=0, tiled=True)  23 us
    reduce_scatter x1, waiting for transfers between devices, local(): lax.psum_scatter(grad_key[0], 'batch', scatter_dimension=0, tiled=True)  21.4 us
    reduce_scatter x1, waiting for transfers between devices, local(): lax.psum_scatter(grad_value[0], 'batch', scatter_dimension=0, tiled=True)  21.4 us
    reduce_scatter x1, waiting for transfers between devices, local(): lax.psum_scatter(grad_mixed[0], 'batch', scatter_dimension=1, tiled=True)  21.3 us
    all_gather x1, blocking collectives, local(): lax.all_gather(new_key.astype(jnp.bfloat16), 'batch', axis=0, tiled=True)  16.1 us
  transfers between devices with their start and end apart: 8, of which 6 were waited for; matrix products, arithmetic and copies ran while one was open for 4% of the time, Pallas kernels for 0%

commit v1 on v0

v1 whole, which is shorter than its diff:
```python
import functools

import jax
import jax.numpy as jnp
from jax import lax
from jax.experimental import pallas as pl
from jax.experimental.pallas import tpu as pltpu
from jax.sharding import PartitionSpec as P

learn_rate = 0.4
hold_rate = 0.9
tile = 128
matrices = ("up", "down", "query", "key", "value", "mixed")
by_rows = {"up": True, "down": False, "query": True, "key": True, "value": True, "mixed": False}
ahead = 2


class Piece:
    def __init__(self, at, rows_cut, share, start, size, other):
        self.at = at
        self.rows_cut = rows_cut
        self.share = share
        self.start = start
        self.size = size
        self.shape = (size, other) if rows_cut else (other, size)

    def tiles(self):
        r, c = self.shape
        h, w = min(tile, r), min(tile, c)
        return [(i, j, h, w) for i in range(0, r, h) for j in range(0, c, w)]

    def span(self, share, i, j, h, w):
        base = share * self.share
        if self.rows_cut:
            return pl.ds(aligned(base + (self.start + i), h), h), pl.ds(j, w)
        return pl.ds(i, h), pl.ds(aligned(base + (self.start + j), w), w)

    def own(self, i, j, h, w):
        if self.rows_cut:
            return pl.ds(self.start + i, h), pl.ds(j, w)
        return pl.ds(i, h), pl.ds(self.start + j, w)


def aligned(place, size):
    return place if isinstance(place, int) else pl.multiple_of(place, size)


def pieces_of(weights):
    def cut(at, parts=1):
        rows_cut = by_rows[matrices[at]]
        r, c = weights[at].shape
        share, other = (r, c) if rows_cut else (c, r)
        if share % (parts * tile):
            parts = 1
        size = share // parts
        return [Piece(at, rows_cut, share, k * size, size, other) for k in range(parts)]

    return cut(2) + cut(3) + cut(0, 2) + cut(1, 2) + cut(4) + cut(5)


def kernel(pieces, n, m, *refs):
    k = len(matrices)
    grads, weights, moments, vec_ref = refs[:k], refs[k : 2 * k], refs[2 * k : 3 * k], refs[3 * k]
    outs = refs[3 * k + 1 : 6 * k + 2]
    copies, news, states, vecs = outs[:k], outs[k : 2 * k], outs[2 * k : 3 * k], outs[3 * k]
    rest = refs[6 * k + 2 :]
    count = len(pieces)
    from_left, from_right = rest[:count], rest[count : 2 * count]
    totals, mine, theirs = rest[2 * count : 3 * count], rest[3 * count : 4 * count], rest[4 * count : 5 * count]
    (
        sent_right,
        sent_left,
        got_left,
        got_right,
        norm_sent,
        norm_got,
        copy_right,
        copy_left,
        copy_from_left,
        copy_from_right,
        vec_sent,
        vec_got,
    ) = rest[5 * count :]
    d = lax.axis_index("batch")
    e = lax.axis_index("cols")
    right, left = (lax.rem(d + 1, n), e), (lax.rem(d + n - 1, n), e)
    half = n // 2
    rate = n ** (-0.5)

    def send(src, dst, send_sem, recv_sem, where):
        return pltpu.make_async_remote_copy(
            src_ref=src,
            dst_ref=dst,
            send_sem=send_sem,
            recv_sem=recv_sem,
            device_id=where,
            device_id_type=pl.DeviceIdType.MESH,
        )

    barrier = pltpu.get_barrier_semaphore()
    for step in range(1, n):
        pl.semaphore_signal(
            barrier, inc=1, device_id=(lax.rem(d + step, n), e), device_id_type=pl.DeviceIdType.MESH
        )
    for step in range(1, m):
        pl.semaphore_signal(
            barrier, inc=1, device_id=(d, lax.rem(e + step, m)), device_id_type=pl.DeviceIdType.MESH
        )
    pl.semaphore_wait(barrier, n + m - 2)

    def hop(p, s, to_right, first):
        piece = pieces[p]
        buffer = (from_left if to_right else from_right)[p]
        sems = (sent_right, got_left) if to_right else (sent_left, got_right)
        if first:
            src = grads[piece.at].at[(0, *piece.span(s, 0, 0, *piece.shape))]
        else:
            src = buffer.at[s]
        where = right if to_right else left
        return send(src, buffer.at[s], sems[0].at[p, s], sems[1].at[p, s], where)

    def start_line(p):
        @pl.when(d == 0)
        def _():
            for s in reversed(range(1, n)):
                hop(p, s, True, True).start()

        @pl.when(d == n - 1)
        def _():
            for s in range(n - 1):
                hop(p, s, False, True).start()

    def relay(p, to_right, when):
        piece = pieces[p]
        buffer = (from_left if to_right else from_right)[p]
        inner = (d > 0) if to_right else (d < n - 1)
        for s in reversed(range(2, n)) if to_right else range(n - 2):
            beyond = (d < s) if to_right else (d > s)

            @pl.when(when & inner & beyond)
            def _():
                hop(p, s, to_right, False).wait_recv()
                for i, j, h, w in piece.tiles():
                    here = (s, pl.ds(i, h), pl.ds(j, w))
                    buffer[here] = buffer[here] + grads[piece.at][(0, *piece.span(s, i, j, h, w))]
                hop(p, s, to_right, False).start()

    def early(p):
        relay(p, True, d < half)
        relay(p, False, d >= half)

    def late(p):
        relay(p, False, d < half)
        relay(p, True, d >= half)

    def norm_copy(p, step):
        return send(
            mine[p],
            theirs[p].at[step - 1],
            norm_sent.at[p, step - 1],
            norm_got.at[p, step - 1],
            (d, lax.rem(e + step, m)),
        )

    def combine(p):
        piece = pieces[p]
        g, w_ref, total = grads[piece.at], weights[piece.at], totals[p]

        @pl.when(d > 0)
        def _():
            hop(p, d, True, False).wait_recv()

        @pl.when(d < n - 1)
        def _():
            hop(p, d, False, False).wait_recv()

        @pl.when(d == 0)
        def _():
            from_left[p][0] = jnp.zeros(piece.shape, jnp.float32)

        @pl.when(d == n - 1)
        def _():
            from_right[p][n - 1] = jnp.zeros(piece.shape, jnp.float32)

        mine[p][...] = jnp.zeros(mine[p].shape, jnp.float32)
        sums = {}
        for i, j, h, w in piece.tiles():
            here = (d, pl.ds(i, h), pl.ds(j, w))
            value = (from_left[p][here] + g[(0, *piece.span(d, i, j, h, w))]) + from_right[p][here]
            value = value * rate
            total[pl.ds(i, h), pl.ds(j, w)] = value
            weight = w_ref[piece.own(i, j, h, w)]
            pair = (weight * weight, value * value)
            if not piece.rows_cut:
                pair = tuple(jnp.sum(x, axis=0, keepdims=True) for x in pair)
            key = i if piece.rows_cut else j
            sums[key] = tuple(a + b for a, b in zip(sums[key], pair)) if key in sums else pair
        for key, pair in sums.items():
            if piece.rows_cut:
                pair = tuple(jnp.sum(x.T, axis=0, keepdims=True) for x in pair)
            for row, x in enumerate(pair):
                mine[p][pl.ds(row, 1), pl.ds(key, x.shape[1])] = x
        for step in range(1, m):
            norm_copy(p, step).start()

    def copy_block(p, owner):
        piece = pieces[p]
        return copies[piece.at].at[piece.span(owner, 0, 0, *piece.shape)]

    def copy_hop(p, k, to_right):
        owner = d - (k - 1) if to_right else d + (k - 1)
        sems = (copy_right, copy_from_left) if to_right else (copy_left, copy_from_right)
        where = right if to_right else left
        block = copy_block(p, owner)
        return send(block, block, sems[0].at[p, k - 1], sems[1].at[p, k - 1], where)

    def copy_wait(p, k, to_right):
        owner = d - k if to_right else d + k
        sems = (copy_right, copy_from_left) if to_right else (copy_left, copy_from_right)
        block = copy_block(p, owner)
        send(block, block, sems[0].at[p, k - 1], sems[1].at[p, k - 1], right).wait_recv()

    def update(p):
        piece = pieces[p]
        for step in range(1, m):
            norm_copy(p, step).wait_recv()
        squares = mine[p][...]
        for step in range(1, m):
            squares = squares + theirs[p][step - 1]
        ratio = jnp.sqrt(squares[0:1]) * lax.rsqrt(squares[1:2] + 1e-06)
        spread = {}
        for i, j, h, w in piece.tiles():
            key = i if piece.rows_cut else j
            if key not in spread:
                if piece.rows_cut:
                    spread[key] = jnp.broadcast_to(ratio[:, i : i + h], (w, h)).T
                else:
                    spread[key] = ratio[:, j : j + w]
            own = piece.own(i, j, h, w)
            mean = totals[p][pl.ds(i, h), pl.ds(j, w)] * spread[key]
            state = hold_rate * moments[piece.at][own] + mean
            new = weights[piece.at][own] - learn_rate * state
            states[piece.at][own] = state
            news[piece.at][own] = new
            copies[piece.at][piece.span(d, i, j, h, w)] = new.astype(jnp.bfloat16)
        hand_on(p, 1)

    def hand_on(p, k):
        @pl.when(d >= k - 1)
        def _():
            if k > 1:
                copy_wait(p, k - 1, True)
            if k < n:

                @pl.when(d < n - 1)
                def _():
                    copy_hop(p, k, True).start()

        @pl.when(d <= n - k)
        def _():
            if k > 1:
                copy_wait(p, k - 1, False)
            if k < n:

                @pl.when(d > 0)
                def _():
                    copy_hop(p, k, False).start()

    def vec_copy(step):
        return send(
            vec_ref,
            vecs.at[d],
            vec_sent.at[step - 1],
            vec_got.at[step - 1],
            (lax.rem(d + step, n), e),
        )

    def vec_from(step):
        source = lax.rem(d - step + n, n)
        return send(vec_ref, vecs.at[source], vec_sent.at[step - 1], vec_got.at[step - 1], (lax.rem(d + step, n), e))

    for p in range(min(ahead, count)):
        start_line(p)
        if p == 0:
            for step in range(1, n):
                vec_copy(step).start()
            vecs[d] = vec_ref[...]
    for t in range(count + 3 + n):
        stages = [(start_line, ahead), (early, 0), (late, -1), (combine, -2), (update, -3)]
        for stage, lag in stages:
            if 0 <= t + lag < count:
                stage(t + lag)
        for k in range(2, n + 1):
            if 0 <= t - 2 - k < count:
                hand_on(t - 2 - k, k)

    for step in range(1, n):
        vec_from(step).wait_recv()
        vec_copy(step).wait_send()
    for p in range(count):
        for s in range(1, n):

            @pl.when(d < s)
            def _():
                hop(p, s, True, False).wait_send()

        for s in range(n - 1):

            @pl.when(d > s)
            def _():
                hop(p, s, False, False).wait_send()

        for step in range(1, m):
            norm_copy(p, step).wait_send()
        for k in range(1, n):

            @pl.when((d >= k - 1) & (d < n - 1))
            def _():
                copy_hop(p, k, True).wait_send()

            @pl.when((d <= n - k) & (d > 0))
            def _():
                copy_hop(p, k, False).wait_send()


def local(*args):
    grads, weights, moments = args[:6], args[8:14], args[16:22]
    grad_vecs, weight_vecs, moment_vecs = args[6:8], args[14:16], args[22:24]
    n, m = lax.axis_size("batch"), lax.axis_size("cols")
    pieces = pieces_of(weights)
    count = len(pieces)
    width = grad_vecs[0].shape[1]
    part = weight_vecs[0].shape[0]

    shares = jnp.concatenate((*weight_vecs, *moment_vecs))
    shares = jnp.pad(shares, (0, width - shares.shape[0]))
    message = jnp.stack((grad_vecs[0][0], grad_vecs[1][0], shares))
    message = jnp.pad(message, ((0, 5), (0, 0)))

    f32 = jnp.float32
    out_shape = (
        [jax.ShapeDtypeStruct(g.shape[1:], jnp.bfloat16) for g in grads]
        + [jax.ShapeDtypeStruct(w.shape, f32) for w in weights] * 2
        + [jax.ShapeDtypeStruct((n, 8, width), f32)]
    )
    scratch = [pltpu.VMEM((n, *p.shape), f32) for p in pieces] * 2
    scratch += [pltpu.VMEM(p.shape, f32) for p in pieces]
    scratch += [pltpu.VMEM((8, max(tile, p.size)), f32) for p in pieces]
    scratch += [pltpu.VMEM((m - 1, 8, max(tile, p.size)), f32) for p in pieces]
    dma = pltpu.SemaphoreType.DMA
    scratch += [dma((count, n))] * 4 + [dma((count, m - 1))] * 2 + [dma((count, n - 1))] * 4
    scratch += [dma((n - 1,))] * 2
    vmem = pl.BlockSpec(memory_space=pltpu.VMEM)
    results = pl.pallas_call(
        functools.partial(kernel, pieces, n, m),
        out_shape=out_shape,
        in_specs=[vmem] * 19,
        out_specs=[vmem] * len(out_shape),
        scratch_shapes=scratch,
        compiler_params=pltpu.CompilerParams(
            collective_id=0, has_side_effects=True, vmem_limit_bytes=60 * 1024 * 1024
        ),
    )(*grads, *weights, *moments, message)
    copies, news, states, vecs = results[:6], results[6:12], results[12:18], results[18]

    whole = vecs[0, :2]
    for s in range(1, n):
        whole = whole + vecs[s, :2]
    mean = whole * n ** (-0.5)
    held = vecs[:, 2, : 4 * part].reshape(n, 2, 2, part).transpose(1, 2, 0, 3).reshape(2, 2, width)
    vec_copy = (held[0] - learn_rate * (hold_rate * held[1] + mean)).astype(jnp.bfloat16)
    place = lax.axis_index("batch")
    own_mean = lax.dynamic_slice_in_dim(mean, place * part, part, axis=1)
    vec_state = [hold_rate * moment_vecs[k] + own_mean[k] for k in range(2)]
    vec_new = [weight_vecs[k] - learn_rate * vec_state[k] for k in range(2)]
    return (*copies, vec_copy[0], vec_copy[1], *news, *vec_new, *states, *vec_state)


def solution(mesh):
    grads = [P("batch", None, "cols") if by_rows[x] else P("batch", "cols", None) for x in matrices]
    held = [P("batch", "cols") if by_rows[x] else P("cols", "batch") for x in matrices]
    whole = [P(None, "cols") if by_rows[x] else P("cols", None) for x in matrices]
    vector = [P("batch")] * 2
    return jax.shard_map(
        local,
        mesh=mesh,
        in_specs=(*grads, P("batch", None), P("batch", None), *held, *vector, *held, *vector),
        out_specs=(*whole, P(), P(), *held, *vector, *held, *vector),
        check_vma=False,
    )
```

time: 326 us -> 190 us (0.58)
  waiting for transfers between devices: 178 us -> 0 us
  Pallas kernels: 0 us -> 169 us
  blocking collectives: 111 us -> 0 us
  between operations: 14.5 us -> 0.75 us
  other arithmetic: 14.2 us -> 3.49 us
  local copies, waits for them, and re-layouts: 7.42 us -> 16.4 us
    reduce_scatter x6 -> x0, waiting for transfers between devices: 174 us -> none  [the longest x1 43.8 us: local(): lax.psum_scatter(grad_down[0], 'batch', scatter_dimension=1, tiled=True)]
    pallas_call x0 -> x1, Pallas kernels: none -> 169 us  [local(): pl.pallas_call(functools.partial(kernel, pieces, n, m), out_shape=out_sha...]
    all_gather x6 -> x0, blocking collectives: 77.2 us -> none  [the longest x1 16.1 us: local(): lax.all_gather(new_key.astype(jnp.bfloat16), 'batch', axis=0, tiled=True)]
    psum x2 -> x0, blocking collectives: 34.1 us -> none  [the longest x1 23.6 us: local(): lax.psum((jnp.sum(weight_up * weight_up, axis=1, keepdims=True), jnp.sum(...]
    unnamed x58 -> x62, local copies, waits for them, and re-layouts: 7.42 us -> 14.6 us
    reduce_sum x12 -> x0, other arithmetic: 6.93 us -> none  [the longest x1 1.24 us: local(): jnp.sum(mean_up * mean_up, axis=1, keepdims=True)]
    convert_element_type x7 -> x1, other arithmetic: 7.22 us -> 0.83 us  [local(): (held[0] - learn_rate * (hold_rate * held[1] + mean)).astype(jnp.bfloat16)]
    unnamed x8 -> x0, waiting for transfers between devices: 3.62 us -> none
  transfers between devices with their start and end apart: 8 -> 0, of which waited for: 6 -> 0; matrix products, arithmetic and copies ran while one was open for 4% -> 0% of each run, Pallas kernels for 0% -> 0%
where the time goes in v1:
time: 190 us
  Pallas kernels  169 us (89%)
  local copies, waits for them, and re-layouts  16.4 us (9%)
  other arithmetic  3.49 us (2%)
    pallas_call x1, Pallas kernels, local(): pl.pallas_call(functools.partial(kernel, pieces, n, m), out_shape=out_sha...  169 us
    unnamed x62, local copies, waits for them, and re-layouts  14.6 us

profile of v1, /device:TPU:0, one launch (start us, length us, event | category | flops | bytes accessed | tf_op | source)
XLA Modules:
  0.0 190.0 jit_solution(5445577341846897773)
XLA Ops:
  0.7 0.7 pad_maximum_fusion
  1.4 1.3 select_maximum_fusion.refs_18_
  2.7 0.0 copy-start.17
  2.7 0.0 copy-start.18
  2.7 0.0 copy-start.20
  2.7 169.4 %shard_map.415 = (bf16[1024,512]{1,0:T(8,128)(2,1)}, bf16[512,1024]{1,0:T(8,128)(2,1)}, bf16[1024,128]{1,0:T(8,128)(2,1)}, bf16[1024,128]{1,0:T(8,128)(2,1)}, bf...) custom-call(f32[1,1024,512]{2,1,0:T(8,128)} %refs_0_.1, ...), custom_call_target="tpu_custom_call" | custom-call | tf_op jit(solution)/shard_map/pallas_call | solution.py:354
  172.2 0.0 copy-start
  172.2 1.0 slice_reduce_fusion
  173.3 0.8 fusion.3
  174.1 0.1 constant_dynamic-slice_fusion.1
  174.2 0.0 copy-done.17
  174.2 0.0 copy-done.18
  174.2 0.0 copy-done.19
  174.2 0.0 copy-done.20
  174.2 0.6 multiply_subtract_fusion
  174.8 0.6 slice_reduce_fusion.1
  175.4 0.0 copy-start.7
  175.4 0.0 copy-start.6
  175.4 2.3 %copy.69 = bf16[1024,512]{1,0:T(8,128)(2,1)} copy(bf16[1024,512]{1,0:T(8,128)(2,1)} %get-tuple-element.100) | data formatting | bytes 2097152
  177.7 0.0 copy-done
  177.8 0.0 copy-start.5
  177.8 0.0 copy-start.4
  177.8 1.0 copy.70
  178.7 0.0 copy-done.8
  178.7 0.0 copy-start.3
  178.7 0.0 copy-start.16
  178.7 0.7 copy.71
  179.4 0.0 copy-done.7
  179.4 0.0 copy-start.15
  179.4 0.0 copy-start.14
  179.4 0.7 copy.72
  180.1 0.0 copy-done.6
  180.1 0.0 copy-start.13
  180.2 0.0 copy-start.2
  180.2 0.7 copy.73
  180.9 0.0 copy-done.5
  180.9 0.7 copy.74
  181.6 0.0 copy-done.4
  181.6 0.0 copy-start.1
  181.6 0.8 copy.75
  182.4 0.0 copy-done.3
  182.4 0.0 copy-start.12
  182.4 0.0 copy-start.11
  182.4 0.8 copy.76
  183.2 0.0 copy-done.16
  183.2 0.7 copy.77
  183.8 0.0 copy-done.15
  183.8 0.7 copy.78
  184.5 0.0 copy-done.14
  184.5 0.7 copy.79
  185.1 0.0 copy-done.13
  185.1 0.7 copy.80
  185.8 0.0 copy-done.2
  185.8 0.8 copy.81
  186.6 0.0 copy-done.1
  186.6 0.8 copy.82
  187.4 0.0 copy-done.12
  187.4 0.7 copy.83
  188.0 0.0 copy-done.11
  188.1 0.7 copy.84
  188.7 0.0 copy-done.10
  188.7 0.7 copy.85
  189.4 0.0 copy-done.9
  189.4 0.7 copy.86
  (7 shorter events, 0.0 us)
Async XLA Ops:
  2.7 171.5 %copy-start.17 = (f32[256]{0:T(256)S(1)}, f32[256]{0:T(256)}, u32[]{:S(2)}) copy-start(f32[256]{0:T(256)} %param.47) | copy-start | bytes 3076
  2.7 171.5 %copy-start.18 = (f32[256]{0:T(256)S(1)}, f32[256]{0:T(256)}, u32[]{:S(2)}) copy-start(f32[256]{0:T(256)} %param.46) | copy-start | bytes 3076
  2.7 171.5 %copy-start.19 = (f32[256]{0:T(256)S(1)}, f32[256]{0:T(256)}, u32[]{:S(2)}) copy-start(f32[256]{0:T(256)} %param.39) | copy-start | bytes 3076
  2.7 171.5 %copy-start.20 = (f32[256]{0:T(256)S(1)}, f32[256]{0:T(256)}, u32[]{:S(2)}) copy-start(f32[256]{0:T(256)} %param.38) | copy-start | bytes 3076
  172.2 5.6 %copy-start = (bf16[512,1024]{1,0:T(8,128)(2,1)S(1)}, bf16[512,1024]{1,0:T(8,128)(2,1)}, u32[]{:S(2)}) copy-start(bf16[512,1024]{1,0:T(8,128)(2,1)} %get-tuple-element.101) | copy-start | bytes 3145732
  175.4 3.3 %copy-start.8 = (bf16[1024,128]{1,0:T(8,128)(2,1)S(1)}, bf16[1024,128]{1,0:T(8,128)(2,1)}, u32[]{:S(2)}) copy-start(bf16[1024,128]{1,0:T(8,128)(2,1)} %get-tuple-element.102) | copy-start | bytes 786436
  175.4 4.0 %copy-start.7 = (bf16[1024,128]{1,0:T(8,128)(2,1)S(1)}, bf16[1024,128]{1,0:T(8,128)(2,1)}, u32[]{:S(2)}) copy-start(bf16[1024,128]{1,0:T(8,128)(2,1)} %get-tuple-element.103) | copy-start | bytes 786436
  175.4 4.7 %copy-start.6 = (bf16[1024,128]{1,0:T(8,128)(2,1)S(1)}, bf16[1024,128]{1,0:T(8,128)(2,1)}, u32[]{:S(2)}) copy-start(bf16[1024,128]{1,0:T(8,128)(2,1)} %get-tuple-element.104) | copy-start | bytes 786436
  177.8 3.1 %copy-start.5 = (bf16[128,1024]{1,0:T(8,128)(2,1)S(1)}, bf16[128,1024]{1,0:T(8,128)(2,1)}, u32[]{:S(2)}) copy-start(bf16[128,1024]{1,0:T(8,128)(2,1)} %get-tuple-element.105) | copy-start | bytes 786436
  177.8 3.8 %copy-start.4 = (f32[256,512]{1,0:T(8,128)S(1)}, f32[256,512]{1,0:T(8,128)}, u32[]{:S(2)}) copy-start(f32[256,512]{1,0:T(8,128)} %get-tuple-element.108) | copy-start | bytes 1572868
  178.7 3.6 %copy-start.3 = (f32[512,256]{1,0:T(8,128)S(1)}, f32[512,256]{1,0:T(8,128)}, u32[]{:S(2)}) copy-start(f32[512,256]{1,0:T(8,128)} %get-tuple-element.109) | copy-start | bytes 1572868
  178.7 4.4 %copy-start.16 = (f32[256,128]{1,0:T(8,128)S(1)}, f32[256,128]{1,0:T(8,128)}, u32[]{:S(2)}) copy-start(f32[256,128]{1,0:T(8,128)} %get-tuple-element.110) | copy-start | bytes 393220
  179.4 4.4 %copy-start.15 = (f32[256,128]{1,0:T(8,128)S(1)}, f32[256,128]{1,0:T(8,128)}, u32[]{:S(2)}) copy-start(f32[256,128]{1,0:T(8,128)} %get-tuple-element.111) | copy-start | bytes 393220
  179.4 5.0 %copy-start.14 = (f32[256,128]{1,0:T(8,128)S(1)}, f32[256,128]{1,0:T(8,128)}, u32[]{:S(2)}) copy-start(f32[256,128]{1,0:T(8,128)} %get-tuple-element.112) | copy-start | bytes 393220
  180.1 5.0 %copy-start.13 = (f32[128,256]{1,0:T(8,128)S(1)}, f32[128,256]{1,0:T(8,128)}, u32[]{:S(2)}) copy-start(f32[128,256]{1,0:T(8,128)} %get-tuple-element.113) | copy-start | bytes 393220
  180.2 5.7 %copy-start.2 = (f32[256,512]{1,0:T(8,128)S(1)}, f32[256,512]{1,0:T(8,128)}, u32[]{:S(2)}) copy-start(f32[256,512]{1,0:T(8,128)} %get-tuple-element.116) | copy-start | bytes 1572868
  181.6 5.0 %copy-start.1 = (f32[512,256]{1,0:T(8,128)S(1)}, f32[512,256]{1,0:T(8,128)}, u32[]{:S(2)}) copy-start(f32[512,256]{1,0:T(8,128)} %get-tuple-element.117) | copy-start | bytes 1572868
  182.4 5.0 %copy-start.12 = (f32[256,128]{1,0:T(8,128)S(1)}, f32[256,128]{1,0:T(8,128)}, u32[]{:S(2)}) copy-start(f32[256,128]{1,0:T(8,128)} %get-tuple-element.118) | copy-start | bytes 393220
  182.4 5.7 %copy-start.11 = (f32[256,128]{1,0:T(8,128)S(1)}, f32[256,128]{1,0:T(8,128)}, u32[]{:S(2)}) copy-start(f32[256,128]{1,0:T(8,128)} %get-tuple-element.119) | copy-start | bytes 393220
  183.2 5.5 %copy-start.10 = (f32[256,128]{1,0:T(8,128)S(1)}, f32[256,128]{1,0:T(8,128)}, u32[]{:S(2)}) copy-start(f32[256,128]{1,0:T(8,128)} %get-tuple-element.120) | copy-start | bytes 393220
  183.2 6.2 %copy-start.9 = (f32[128,256]{1,0:T(8,128)S(1)}, f32[128,256]{1,0:T(8,128)}, u32[]{:S(2)}) copy-start(f32[128,256]{1,0:T(8,128)} %get-tuple-element.121) | copy-start | bytes 393220

commit v2 on v1

--- a/solution.py
+++ b/solution.py
@@ -61,9 +61,9 @@
 def kernel(pieces, n, m, *refs):
     k = len(matrices)
     grads, weights, moments, vec_ref = refs[:k], refs[k : 2 * k], refs[2 * k : 3 * k], refs[3 * k]
-    outs = refs[3 * k + 1 : 6 * k + 2]
-    copies, news, states, vecs = outs[:k], outs[k : 2 * k], outs[2 * k : 3 * k], outs[3 * k]
-    rest = refs[6 * k + 2 :]
+    outs = refs[3 * k + 1 : 5 * k + 2]
+    copies, means, vecs = outs[:k], outs[k : 2 * k], outs[2 * k]
+    rest = refs[5 * k + 2 :]
     count = len(pieces)
     from_left, from_right = rest[:count], rest[count : 2 * count]
     totals, mine, theirs = rest[2 * count : 3 * count], rest[3 * count : 4 * count], rest[4 * count : 5 * count]
@@ -240,8 +240,7 @@
             mean = totals[p][pl.ds(i, h), pl.ds(j, w)] * spread[key]
             state = hold_rate * moments[piece.at][own] + mean
             new = weights[piece.at][own] - learn_rate * state
-            states[piece.at][own] = state
-            news[piece.at][own] = new
+            means[piece.at][own] = mean
             copies[piece.at][piece.span(d, i, j, h, w)] = new.astype(jnp.bfloat16)
         hand_on(p, 1)
 
@@ -291,8 +290,8 @@
             if 0 <= t + lag < count:
                 stage(t + lag)
         for k in range(2, n + 1):
-            if 0 <= t - 2 - k < count:
-                hand_on(t - 2 - k, k)
+            if 0 <= t - 3 - k < count:
+                hand_on(t - 3 - k, k)
 
     for step in range(1, n):
         vec_from(step).wait_recv()
@@ -340,7 +339,7 @@
     f32 = jnp.float32
     out_shape = (
         [jax.ShapeDtypeStruct(g.shape[1:], jnp.bfloat16) for g in grads]
-        + [jax.ShapeDtypeStruct(w.shape, f32) for w in weights] * 2
+        + [jax.ShapeDtypeStruct(w.shape, f32) for w in weights]
         + [jax.ShapeDtypeStruct((n, 8, width), f32)]
     )
     scratch = [pltpu.VMEM((n, *p.shape), f32) for p in pieces] * 2
@@ -361,7 +360,9 @@
             collective_id=0, has_side_effects=True, vmem_limit_bytes=60 * 1024 * 1024
         ),
     )(*grads, *weights, *moments, message)
-    copies, news, states, vecs = results[:6], results[6:12], results[12:18], results[18]
+    copies, means, vecs = results[:6], results[6:12], results[12]
+    states = [hold_rate * x + mean for x, mean in zip(moments, means)]
+    news = [x - learn_rate * state for x, state in zip(weights, states)]
 
     whole = vecs[0, :2]
     for s in range(1, n):

time: 190 us -> 182 us (0.958)
  local copies, waits for them, and re-layouts: 16.4 us -> 6.65 us
  other arithmetic: 3.49 us -> 9.07 us
  Pallas kernels: 169 us -> 165 us
    unnamed x62, local copies, waits for them, and re-layouts: 14.6 us -> 4.89 us
    sub x0 -> x5, other arithmetic: none -> 5.58 us  [local(): news = [x - learn_rate * state for x, state in zip(weights, states)]]
    pallas_call x1, Pallas kernels: 169 us -> 165 us  [local(): pl.pallas_call(functools.partial(kernel, pieces, n, m), out_shape=out_sha...]
where the time goes in v2:
time: 182 us; the launch traced here: 181 us
  Pallas kernels  165 us (91%)
  other arithmetic  9.07 us (5%)
  local copies, waits for them, and re-layouts  6.65 us (4%)
    pallas_call x1, Pallas kernels, local(): pl.pallas_call(functools.partial(kernel, pieces, n, m), out_shape=out_sha...  165 us
    sub x5, other arithmetic, local(): news = [x - learn_rate * state for x, state in zip(weights, states)]  5.58 us
    unnamed x62, local copies, waits for them, and re-layouts  4.89 us

profile of v2, /device:TPU:0, one launch (start us, length us, event | category | flops | bytes accessed | tf_op | source)
XLA Modules:
  0.0 181.4 jit_solution(12311773897572540375)
XLA Ops:
  0.7 0.7 pad_maximum_fusion
  1.4 1.3 select_maximum_fusion.refs_18_
  2.7 0.0 copy-start
  2.7 0.0 copy-start.1
  2.7 164.7 %shard_map.415 = (bf16[1024,512]{1,0:T(8,128)(2,1)}, bf16[512,1024]{1,0:T(8,128)(2,1)}, bf16[1024,128]{1,0:T(8,128)(2,1)}, bf16[1024,128]{1,0:T(8,128)(2,1)}, bf...) custom-call(f32[1,1024,512]{2,1,0:T(8,128)} %refs_0_.1, ...), custom_call_target="tpu_custom_call" | custom-call | tf_op jit(solution)/shard_map/pallas_call | solution.py:353
  167.5 0.0 copy-start.2
  167.5 0.0 copy-start.3
  167.5 0.0 copy-start.14
  167.5 1.1 slice_reduce_fusion
  168.6 0.8 fusion.3
  169.5 0.6 slice_reduce_fusion.1
  170.1 0.0 copy-done
  170.1 0.0 copy-done.1
  170.1 0.0 copy-start.6
  170.1 0.0 copy-start.7
  170.1 0.0 copy-start.22
  170.1 2.2 %multiply_subtract_fusion.1 = (f32[256,512]{1,0:T(8,128)}, f32[256,512]{1,0:T(8,128)}) fusion(f32[256,512]{1,0:T(8,128)S(1)} %copy-done, f32[256,512]{1,0:T(8,128)} %get-tuple-element.44, f32[256,512]{1,0:T(8,128)S(1)} %copy-done.1), kind=kLoop, calls=%fused_computation.2 | loop fusion | flops 524288 | bytes 2621440 | tf_op jit(solution)/shard_map/sub | solution.py:365
  172.3 0.0 copy-start.20
  172.3 0.0 copy-start.21
  172.4 0.0 copy-done.2
  172.4 0.0 copy-done.3
  172.4 0.0 copy-done.14
  172.4 0.0 copy-start.12
  172.4 0.0 copy-start.13
  172.4 0.0 copy-start.19
  172.4 0.0 copy-start.23
  172.4 0.0 copy-start.24
  172.4 0.0 copy-start.25
  172.5 0.0 copy-start.26
  172.5 0.0 copy-start.5
  172.5 1.1 multiply_subtract_fusion
  173.6 0.0 copy-done.6
  173.6 0.0 copy-done.7
  173.6 0.0 copy-done.22
  173.6 0.7 multiply_subtract_fusion.5
  174.3 0.0 copy-done.8
  174.3 0.0 copy-done.9
  174.3 0.0 copy-done.10
  174.3 0.0 copy-done.11
  174.3 0.0 copy-done.20
  174.3 0.0 copy-done.21
  174.3 0.8 multiply_subtract_fusion.3
  175.2 0.0 copy-done.12
  175.2 0.0 copy-done.13
  175.2 0.0 copy-done.19
  175.2 0.7 multiply_subtract_fusion.2
  175.9 0.1 constant_dynamic-slice_fusion.1
  176.0 0.0 copy-done.23
  176.0 0.0 copy-done.24
  176.0 0.0 copy-done.25
  176.0 0.0 copy-done.26
  176.0 0.6 multiply_subtract_fusion.6
  176.6 0.0 copy-done.5
  176.6 1.0 copy.57
  177.6 0.0 copy-done.4
  177.6 1.0 copy.58
  178.5 0.0 copy-done.18
  178.5 0.7 copy.59
  179.2 0.0 copy-done.17
  179.2 0.7 copy.60
  179.9 0.0 copy-done.16
  180.0 0.7 copy.61
  180.7 0.0 copy-done.15
  180.7 0.7 copy.62
  (12 shorter events, 0.0 us)
Async XLA Ops:
  2.7 167.3 %copy-start = (f32[256,512]{1,0:T(8,128)S(1)}, f32[256,512]{1,0:T(8,128)}, u32[]{:S(2)}) copy-start(f32[256,512]{1,0:T(8,128)} %refs_6_.1) | copy-start | bytes 1572868
  2.7 167.3 %copy-start.1 = (f32[256,512]{1,0:T(8,128)S(1)}, f32[256,512]{1,0:T(8,128)}, u32[]{:S(2)}) copy-start(f32[256,512]{1,0:T(8,128)} %refs_12_.1) | copy-start | bytes 1572868
  167.5 4.9 %copy-start.2 = (f32[512,256]{1,0:T(8,128)S(1)}, f32[512,256]{1,0:T(8,128)}, u32[]{:S(2)}) copy-start(f32[512,256]{1,0:T(8,128)} %refs_7_.1) | copy-start | bytes 1572868
  167.5 4.9 %copy-start.3 = (f32[512,256]{1,0:T(8,128)S(1)}, f32[512,256]{1,0:T(8,128)}, u32[]{:S(2)}) copy-start(f32[512,256]{1,0:T(8,128)} %refs_13_.1) | copy-start | bytes 1572868
  167.5 4.9 %copy-start.14 = (f32[512,256]{1,0:T(8,128)S(1)}, f32[512,256]{1,0:T(8,128)}, u32[]{:S(2)}) copy-start(f32[512,256]{1,0:T(8,128)} %get-tuple-element.45) | copy-start | bytes 1572868
  170.1 3.5 %copy-start.6 = (f32[256,128]{1,0:T(8,128)S(1)}, f32[256,128]{1,0:T(8,128)}, u32[]{:S(2)}) copy-start(f32[256,128]{1,0:T(8,128)} %refs_8_.1) | copy-start | bytes 393220
  170.1 3.5 %copy-start.7 = (f32[256,128]{1,0:T(8,128)S(1)}, f32[256,128]{1,0:T(8,128)}, u32[]{:S(2)}) copy-start(f32[256,128]{1,0:T(8,128)} %refs_14_.1) | copy-start | bytes 393220
  170.1 3.5 %copy-start.22 = (f32[256,128]{1,0:T(8,128)S(1)}, f32[256,128]{1,0:T(8,128)}, u32[]{:S(2)}) copy-start(f32[256,128]{1,0:T(8,128)} %get-tuple-element.46) | copy-start | bytes 393220
  172.3 2.0 %copy-start.8 = (f32[256,128]{1,0:T(8,128)S(1)}, f32[256,128]{1,0:T(8,128)}, u32[]{:S(2)}) copy-start(f32[256,128]{1,0:T(8,128)} %refs_9_.1) | copy-start | bytes 393220
  172.3 2.0 %copy-start.9 = (f32[256,128]{1,0:T(8,128)S(1)}, f32[256,128]{1,0:T(8,128)}, u32[]{:S(2)}) copy-start(f32[256,128]{1,0:T(8,128)} %refs_10_.1) | copy-start | bytes 393220
  172.3 2.0 %copy-start.10 = (f32[256,128]{1,0:T(8,128)S(1)}, f32[256,128]{1,0:T(8,128)}, u32[]{:S(2)}) copy-start(f32[256,128]{1,0:T(8,128)} %refs_15_.1) | copy-start | bytes 393220
  172.3 2.0 %copy-start.11 = (f32[256,128]{1,0:T(8,128)S(1)}, f32[256,128]{1,0:T(8,128)}, u32[]{:S(2)}) copy-start(f32[256,128]{1,0:T(8,128)} %refs_16_.1) | copy-start | bytes 393220
  172.3 2.0 %copy-start.20 = (f32[256,128]{1,0:T(8,128)S(1)}, f32[256,128]{1,0:T(8,128)}, u32[]{:S(2)}) copy-start(f32[256,128]{1,0:T(8,128)} %get-tuple-element.47) | copy-start | bytes 393220
  172.3 2.0 %copy-start.21 = (f32[256,128]{1,0:T(8,128)S(1)}, f32[256,128]{1,0:T(8,128)}, u32[]{:S(2)}) copy-start(f32[256,128]{1,0:T(8,128)} %get-tuple-element.48) | copy-start | bytes 393220
  172.4 2.8 %copy-start.12 = (f32[128,256]{1,0:T(8,128)S(1)}, f32[128,256]{1,0:T(8,128)}, u32[]{:S(2)}) copy-start(f32[128,256]{1,0:T(8,128)} %refs_11_.1) | copy-start | bytes 393220
  172.4 2.8 %copy-start.13 = (f32[128,256]{1,0:T(8,128)S(1)}, f32[128,256]{1,0:T(8,128)}, u32[]{:S(2)}) copy-start(f32[128,256]{1,0:T(8,128)} %refs_17_.1) | copy-start | bytes 393220
  172.4 2.8 %copy-start.19 = (f32[128,256]{1,0:T(8,128)S(1)}, f32[128,256]{1,0:T(8,128)}, u32[]{:S(2)}) copy-start(f32[128,256]{1,0:T(8,128)} %get-tuple-element.49) | copy-start | bytes 393220
  172.4 3.6 %copy-start.23 = (f32[256]{0:T(256)S(1)}, f32[256]{0:T(256)}, u32[]{:S(2)}) copy-start(f32[256]{0:T(256)} %param.47) | copy-start | bytes 3076
  172.4 3.5 %copy-start.24 = (f32[256]{0:T(256)S(1)}, f32[256]{0:T(256)}, u32[]{:S(2)}) copy-start(f32[256]{0:T(256)} %param.46) | copy-start | bytes 3076
  172.4 3.5 %copy-start.25 = (f32[256]{0:T(256)S(1)}, f32[256]{0:T(256)}, u32[]{:S(2)}) copy-start(f32[256]{0:T(256)} %param.39) | copy-start | bytes 3076
  172.5 3.5 %copy-start.26 = (f32[256]{0:T(256)S(1)}, f32[256]{0:T(256)}, u32[]{:S(2)}) copy-start(f32[256]{0:T(256)} %param.38) | copy-start | bytes 3076
  172.5 4.1 %copy-start.5 = (bf16[1024,512]{1,0:T(8,128)(2,1)S(1)}, bf16[1024,512]{1,0:T(8,128)(2,1)}, u32[]{:S(2)}) copy-start(bf16[1024,512]{1,0:T(8,128)(2,1)} %get-tuple-element.102) | copy-start | bytes 3145732
  174.3 3.3 %copy-start.4 = (bf16[512,1024]{1,0:T(8,128)(2,1)S(1)}, bf16[512,1024]{1,0:T(8,128)(2,1)}, u32[]{:S(2)}) copy-start(bf16[512,1024]{1,0:T(8,128)(2,1)} %get-tuple-element.103) | copy-start | bytes 3145732
  176.6 2.0 %copy-start.18 = (bf16[1024,128]{1,0:T(8,128)(2,1)S(1)}, bf16[1024,128]{1,0:T(8,128)(2,1)}, u32[]{:S(2)}) copy-start(bf16[1024,128]{1,0:T(8,128)(2,1)} %get-tuple-element.104) | copy-start | bytes 786436
  176.6 2.7 %copy-start.17 = (bf16[1024,128]{1,0:T(8,128)(2,1)S(1)}, bf16[1024,128]{1,0:T(8,128)(2,1)}, u32[]{:S(2)}) copy-start(bf16[1024,128]{1,0:T(8,128)(2,1)} %get-tuple-element.105) | copy-start | bytes 786436
  177.6 2.4 %copy-start.16 = (bf16[1024,128]{1,0:T(8,128)(2,1)S(1)}, bf16[1024,128]{1,0:T(8,128)(2,1)}, u32[]{:S(2)}) copy-start(bf16[1024,128]{1,0:T(8,128)(2,1)} %get-tuple-element.106) | copy-start | bytes 786436
  177.6 3.1 %copy-start.15 = (bf16[128,1024]{1,0:T(8,128)(2,1)S(1)}, bf16[128,1024]{1,0:T(8,128)(2,1)}, u32[]{:S(2)}) copy-start(bf16[128,1024]{1,0:T(8,128)(2,1)} %get-tuple-element.107) | copy-start | bytes 786436
